TPU v7x, 32 devices: a whole 2x2x4 slice. The times are simulated.
32 devices in a mesh: dp: 8 (over y, x, core), mp: 4 (over z).
Axes of the slice: x: 2, y: 2, z: 4, core: 2. Of those that a mesh axis runs over, the one named last changes fastest.
Arguments:
- hidden_rows: bfloat16 [4096, 3584], P('dp'), may hold values from -6 to 6
- key_grad: bfloat16 [4096, 512], P('dp', 'mp'), may hold values from -6 to 6
- value_grad: bfloat16 [4096, 512], P('dp', 'mp'), may hold values from -6 to 6
- visual_rows: bfloat16 [2048, 1024], P('dp'), may hold values from -6 to 6
- visual_cotangent: bfloat16 [8, 4, 64, 3584], P('dp'), may hold values from -6 to 6
- norm_gain: float32 [1024], replicated, may hold values from 0.25 to 1.75
- norm_bias: float32 [1024], replicated, may hold values from -3 to 3
- fc1_weight: bfloat16 [1024, 4096], P(None, 'mp'), may hold values from -0.1875 to 0.1875
- fc1_bias: float32 [4096], P('mp'), may hold values from -3 to 3
- fc2_weight: bfloat16 [4096, 1024], P('mp'), may hold values from -0.09375 to 0.09375
- fc2_bias: float32 [1024], replicated, may hold values from -3 to 3
- layer_scale: float32 [1024], replicated, may hold values from 0.3 to 1.5
- token_counts: int32 [8, 8], P('dp'), may hold values from 1 to 32, as said below
- dest_offsets: int32 [8, 8], P('dp'), may hold values from 1 to 4, as said below
Outputs:
- key_weight_grad: float32 [3592, 512], P('dp', 'mp')
- value_weight_grad: float32 [3592, 512], P('dp', 'mp')
- projector_grad: float32 [3592, 1024], P('dp', 'mp')
- handoff: bfloat16 [8, 4, 64, 1024], P('dp', None, None, 'mp')
Inputs may be any that keep to these rules, and one draw needn't show every extreme that they name: `token_counts`: on every data rank the images of one distance, chosen per rank, all have 32 rows. `dest_offsets`: every data rank sends exactly 2 images to each distance from 1 to 4.
All inputs are finite; a program needn't handle non-finite values.
Results may differ from a plain program's by a relative error of at most 0.0046.
Values may be sent and summed in bfloat16 or wider, within the bound.
A program may use at most 64 MiB of HBM per device.

v0:
```python
import functools

import jax
import jax.numpy as jnp
from jax import lax
from jax.experimental import pallas as pl
from jax.experimental.pallas import tpu as pltpu
from jax.sharding import PartitionSpec as P

MESH = pl.DeviceIdType.MESH
BF = jnp.bfloat16
F32 = jnp.float32


def up(x, m):
    return -(-x // m) * m


def factors(n):
    core = 2 if n % 2 == 0 else 1
    rest = n // core
    inner = max(f for f in range(1, rest + 1) if rest % f == 0 and f * f <= rest)
    return core, inner, rest // inner


def erf_gelu(x):
    return 0.5 * x * (1.0 + lax.erf(x * (0.5**0.5)))


def kernel(
    cfg,
    hid_h, key_h, val_h, vis_h, cot_h, fc1_h, fc2_h,
    gain, beta, fc1_b, fc2_b, scale, counts, offsets,
    key_o, val_o, proj_o, hand_o,
    hid, key, val, vis, cot, fc1, fc2,
    big_k, big_v, big_c,
    cot_send, cot_recv,
    k0, k0r, k1, k1r, k2, k2r,
    v0, v0r, v1, v1r, v2, v2r,
    z_send, z_recv, gath,
    load_sem, cot_ss, cot_rs, z_ss, z_rs,
    k0_s, k0_r, k1_s, k1_r, k2_s, k2_r,
    v0_s, v0_r, v1_s, v1_r, v2_s, v2_r,
    g_s, g_r, f_s, f_r,
):
    n, mp, shard, rows_pad, spread, cap = cfg
    nc, na, nb = factors(n)
    me = lax.axis_index("dp")
    col = lax.axis_index("mp")
    dc = lax.rem(me, nc)
    da = lax.rem(lax.div(me, nc), na)
    db = lax.div(me, nc * na)
    tokens, width = hid.shape
    slots = cot.shape[0]
    kc = key.shape[1]
    fcol = hand_o.shape[1]

    def rank(c, a, b):
        return (b * na + a) * nc + c

    loads = []
    for i, (src, dst) in enumerate(
        ((cot_h, cot), (vis_h, vis), (fc1_h, fc1), (fc2_h, fc2), (hid_h, hid), (key_h, key), (val_h, val))
    ):
        cp = pltpu.make_async_copy(src, dst, load_sem.at[i])
        cp.start()
        loads.append(cp)
    barrier = pltpu.get_barrier_semaphore()
    for j in range(1, n):
        pl.semaphore_signal(barrier, inc=1, device_id={"dp": lax.rem(me + j, n)}, device_id_type=MESH)
    for j in range(1, mp):
        pl.semaphore_signal(barrier, inc=1, device_id={"mp": lax.rem(col + j, mp)}, device_id_type=MESH)

    def remote(src, dst, ss, rs, where):
        cp = pltpu.make_async_remote_copy(
            src_ref=src, dst_ref=dst, send_sem=ss, recv_sem=rs, device_id=where, device_id_type=MESH
        )
        cp.start()
        return cp

    step = 512 if width % 512 == 0 else 128

    loads[0].wait()
    half = 128

    def turn(i, _):
        at = pl.multiple_of(i * step, step)
        for h in range(slots // half):
            piece = cot[h * half : (h + 1) * half, pl.ds(at, step)].astype(F32)
            big_c[h, pl.ds(at, step), :] = piece.T
        return 0

    lax.fori_loop(0, width // step, turn, 0)
    tail = big_c.shape[1] - width
    big_c[:, width:, :] = jnp.zeros((slots // half, tail, half), F32)
    for r in range(n):
        for h in range(slots // half):
            cot_send[r, :, h * half : (h + 1) * half] = big_c[h, r * shard : r * shard + rows_pad, :].astype(BF)
    pl.semaphore_wait(barrier, n - 1 + mp - 1)
    cot_cps = []

    def send_cot():
        for j in range(1, n):
            to = lax.rem(me + j, n)
            cot_cps.append(remote(cot_send.at[to], cot_recv.at[j - 1], cot_ss.at[j - 1], cot_rs.at[j - 1], {"dp": to}))

    send_cot()

    loads[1].wait()
    values = vis[...].astype(F32)
    center = jnp.mean(values, axis=1, keepdims=True)
    cen = values - center
    var = jnp.mean(cen * cen, axis=1, keepdims=True)
    normed = (cen * lax.rsqrt(var + 1e-06) * gain[...] + beta[...]).astype(BF)
    loads[2].wait()
    hidden = erf_gelu(jnp.dot(normed, fc1[...], preferred_element_type=F32) + fc1_b[...]).astype(BF)
    loads[3].wait()

    def feat(i):
        return pl.ds(pl.multiple_of(i * fcol, 128), fcol)

    z_cps = []
    order = sorted(range(1, mp), key=lambda j: abs(j - mp / 2))
    for j in order:
        to = lax.rem(col + j, mp)
        z_send[j - 1] = jnp.dot(hidden, fc2[:, feat(to)], preferred_element_type=F32).astype(BF)
        z_cps.append(remote(z_send.at[j - 1], z_recv.at[j - 1], z_ss.at[j - 1], z_rs.at[j - 1], {"mp": to}))
    own = jnp.dot(hidden, fc2[:, feat(col)], preferred_element_type=F32)

    for cp in loads[4:]:
        cp.wait()
    kv = jnp.concatenate([key[...], val[...]], axis=1)

    def product(i, _):
        at = pl.multiple_of(i * step, step)
        res = lax.dot_general(hid[:, pl.ds(at, step)], kv, (((0,), (0,)), ((), ())), preferred_element_type=F32)
        big_k[pl.ds(at, step), :] = res[:, :kc]
        big_v[pl.ds(at, step), :] = res[:, kc:]
        return 0

    lax.fori_loop(0, width // step, product, 0)
    first = lax.broadcasted_iota(jnp.int32, (tail, kc), 0) == 0
    big_k[width:, :] = jnp.where(first, jnp.sum(key[...].astype(F32), axis=0, keepdims=True), 0.0)
    big_v[width:, :] = jnp.where(first, jnp.sum(val[...].astype(F32), axis=0, keepdims=True), 0.0)
    for r in range(n):
        c, a, b = r % nc, (r // nc) % na, r // (nc * na)
        k0[c, a, b] = big_k[r * shard : r * shard + rows_pad, :].astype(BF)
        v0[c, b, a] = big_v[r * shard : r * shard + rows_pad, :].astype(BF)

    def exchange(buf, got, ss, rs, digit, q, peer_of):
        cps = []
        for j in range(1, q):
            to = lax.rem(digit + j, q)
            cps.append(remote(buf.at[to], got.at[j - 1], ss.at[j - 1], rs.at[j - 1], {"dp": peer_of(to)}))
        return cps

    def added(buf, got, digit, q, at):
        total = buf[(digit,) + at].astype(F32)
        for j in range(1, q):
            total = total + got[(j - 1,) + at].astype(F32)
        return total

    at_c = lambda c: rank(c, da, db)
    at_a = lambda a: rank(dc, a, db)
    at_b = lambda b: rank(dc, da, b)
    s0k = exchange(k0, k0r, k0_s, k0_r, dc, nc, at_c)
    s0v = exchange(v0, v0r, v0_s, v0_r, dc, nc, at_c)

    rows = vis.shape[0]
    images = counts.shape[1]
    place = lax.broadcasted_iota(jnp.int32, (1, rows), 1)
    target = jnp.full((1, rows), -1, jnp.int32)
    start = jnp.int32(0)
    for i in range(images):
        cnt, off = counts[0, i], offsets[0, i]
        before = jnp.int32(0)
        for e in range(i):
            before = before + jnp.where(offsets[0, e] == off, counts[0, e], 0)
        inside = (place >= start) & (place < start + cnt)
        target = jnp.where(inside, (off - 1) * cap + before + place - start, target)
        start = start + cnt
    slot_id = lax.broadcasted_iota(jnp.int32, (spread * cap, rows), 0)
    select = jnp.where(slot_id == target, 1.0, 0.0).astype(BF)

    for cp in s0k:
        cp.wait_recv()
    for a in range(na):
        for b in range(nb):
            k1[a, b] = added(k0, k0r, dc, nc, (a, b)).astype(BF)
    s1k = exchange(k1, k1r, k1_s, k1_r, da, na, at_a)
    for cp in s0v:
        cp.wait_recv()
    for b in range(nb):
        for a in range(na):
            v1[b, a] = added(v0, v0r, dc, nc, (b, a)).astype(BF)
    s1v = exchange(v1, v1r, v1_s, v1_r, db, nb, at_b)

    for cp in z_cps:
        cp.wait_recv()
    summed = own
    for j in range(1, mp):
        summed = summed + z_recv[j - 1].astype(F32)
    encoded = (
        vis[:, feat(col)].astype(F32) + scale[:, feat(col)] * (summed + fc2_b[:, feat(col)])
    ).astype(BF)
    gath[me] = jnp.dot(select, encoded, preferred_element_type=F32).astype(BF)
    chips = n // nc
    chip = lax.div(me, nc)
    g_cps, f_cps = [], []
    for j in range(1, nc):
        f_cps.append(
            remote(gath.at[me], gath.at[me], f_s.at[0, j - 1], f_r.at[0, j - 1], {"dp": at_c(lax.rem(dc + j, nc))})
        )
    for j in range(1, chips):
        to = lax.rem(chip + j, chips) * nc + dc
        g_cps.append(remote(gath.at[me], gath.at[me], g_s.at[j - 1], g_r.at[j - 1], {"dp": to}))

    for cp in s1k:
        cp.wait_recv()
    for b in range(nb):
        k2[b] = added(k1, k1r, da, na, (b,)).astype(BF)
    s2k = exchange(k2, k2r, k2_s, k2_r, db, nb, at_b)
    for cp in s1v:
        cp.wait_recv()
    for a in range(na):
        v2[a] = added(v1, v1r, db, nb, (a,)).astype(BF)
    s2v = exchange(v2, v2r, v2_s, v2_r, da, na, at_a)

    for j in range(1, chips):
        g_cps[j - 1].wait_recv()
        source = lax.rem(chip + chips - j, chips) * nc + dc
        for i in range(1, nc):
            f_cps.append(
                remote(
                    gath.at[source], gath.at[source], f_s.at[j, i - 1], f_r.at[j, i - 1],
                    {"dp": at_c(lax.rem(dc + i, nc))},
                )
            )
    for cp in f_cps:
        cp.wait_recv()

    def received(r):
        parts = []
        for k in range(1, spread + 1):
            source = lax.rem(r + n - k, n)
            parts.append(gath[source, (k - 1) * cap : k * cap, :])
        return jnp.concatenate(parts, axis=0)

    mine = received(me)
    hand_o[...] = mine
    total = jnp.dot(cot_send[me], mine, preferred_element_type=F32)
    for j in range(1, n):
        cot_cps[j - 1].wait_recv()
        total = total + jnp.dot(
            cot_recv[j - 1], received(lax.rem(me + n - j, n)), preferred_element_type=F32
        )
    proj_o[...] = total[:shard]

    for cp in s2k:
        cp.wait_recv()
    key_o[...] = added(k2, k2r, db, nb, ())[:shard]
    for cp in s2v:
        cp.wait_recv()
    val_o[...] = added(v2, v2r, da, na, ())[:shard]
    for cp in cot_cps + z_cps + s0k + s0v + s1k + s1v + s2k + s2v + g_cps + f_cps:
        cp.wait_send()


def finish(*refs):
    half = len(refs) // 2
    for src, dst in zip(refs[:half], refs[half:]):
        dst[...] = src[...]


def per_device(
    n, mp, hidden_rows, key_grad, value_grad, visual_rows, visual_cotangent, norm_gain, norm_bias,
    fc1_weight, fc1_bias, fc2_weight, fc2_bias, layer_scale, token_counts, dest_offsets,
):
    tokens, width = hidden_rows.shape
    spread, cap = visual_cotangent.shape[1:3]
    slots = spread * cap
    shard = (width + n) // n
    rp = up(shard, 16)
    nc, na, nb = factors(n)
    kc = key_grad.shape[1]
    rows, feats = visual_rows.shape
    fcol = feats // mp
    tall = up(max((n - 1) * shard + rp, width + 8), 8)
    any_spec = pl.BlockSpec(memory_space=pl.ANY)
    vm = pl.BlockSpec(memory_space=pltpu.VMEM)
    sm = pl.BlockSpec(memory_space=pltpu.SMEM)
    dma = lambda *s: pltpu.SemaphoreType.DMA(tuple(max(x, 1) for x in s))

    def stages(q1, q2):
        return [
            pltpu.VMEM((nc, q1, q2, rp, kc), BF),
            pltpu.VMEM((max(nc - 1, 1), q1, q2, rp, kc), BF),
            pltpu.VMEM((q1, q2, rp, kc), BF),
            pltpu.VMEM((max(q1 - 1, 1), q2, rp, kc), BF),
            pltpu.VMEM((q2, rp, kc), BF),
            pltpu.VMEM((max(q2 - 1, 1), rp, kc), BF),
        ]

    def stage_sems(q1, q2):
        return [dma(q - 1) for q in (nc, nc, q1, q1, q2, q2)]

    outs = pl.pallas_call(
        functools.partial(kernel, (n, mp, shard, rp, spread, cap)),
        out_shape=(
            jax.ShapeDtypeStruct((shard, kc), F32),
            jax.ShapeDtypeStruct((shard, kc), F32),
            jax.ShapeDtypeStruct((shard, fcol), F32),
            jax.ShapeDtypeStruct((slots, fcol), BF),
        ),
        in_specs=[any_spec] * 7 + [vm] * 5 + [sm] * 2,
        out_specs=(vm, vm, vm, vm),
        scratch_shapes=[
            pltpu.VMEM(x.shape, BF)
            for x in (hidden_rows, key_grad, value_grad, visual_rows)
        ]
        + [
            pltpu.VMEM((slots, width), BF),
            pltpu.VMEM(fc1_weight.shape, BF),
            pltpu.VMEM(fc2_weight.shape, BF),
            pltpu.VMEM((tall, kc), F32),
            pltpu.VMEM((tall, kc), F32),
            pltpu.VMEM((slots // 128, tall, 128), F32),
            pltpu.VMEM((n, rp, slots), BF),
            pltpu.VMEM((n - 1, rp, slots), BF),
        ]
        + stages(na, nb)
        + stages(nb, na)
        + [
            pltpu.VMEM((mp - 1, rows, fcol), BF),
            pltpu.VMEM((mp - 1, rows, fcol), BF),
            pltpu.VMEM((n, slots, fcol), BF),
            dma(7), dma(n - 1), dma(n - 1), dma(mp - 1), dma(mp - 1),
        ]
        + stage_sems(na, nb)
        + stage_sems(nb, na)
        + [dma(n // nc - 1), dma(n // nc - 1), dma(n // nc, nc - 1), dma(n // nc, nc - 1)],
        compiler_params=pltpu.CompilerParams(
            collective_id=0, has_side_effects=True, vmem_limit_bytes=60 * 1024 * 1024
        ),
    )(
        hidden_rows, key_grad, value_grad, visual_rows, visual_cotangent.reshape(slots, width),
        fc1_weight, fc2_weight, norm_gain[None], norm_bias[None], fc1_bias[None], fc2_bias[None],
        layer_scale[None], token_counts, dest_offsets,
    )
    outs = pl.pallas_call(
        finish,
        out_shape=tuple(jax.ShapeDtypeStruct(x.shape, x.dtype) for x in outs),
        in_specs=[vm] * 4,
        out_specs=(vm,) * 4,
    )(*outs)
    return outs[0], outs[1], outs[2], outs[3].reshape(1, spread, cap, fcol)


def solution(mesh):
    placed = (
        P("dp", None), P("dp", "mp"), P("dp", "mp"), P("dp", None), P("dp", None, None, None),
        P(), P(), P(None, "mp"), P("mp"), P("mp", None), P(), P(), P("dp", None), P("dp", None),
    )
    return jax.shard_map(
        functools.partial(per_device, mesh.shape["dp"], mesh.shape["mp"]),
        mesh=mesh,
        in_specs=placed,
        out_specs=(P("dp", "mp"), P("dp", "mp"), P("dp", "mp"), P("dp", None, None, "mp")),
        check_vma=False,
    )
```

profile of v0, /device:TPU:1, one launch (start us, length us, event | category | flops | bytes accessed | tf_op | source)
XLA Modules:
  0.0 47.0 jit_solution(11370223513239082711)
XLA Ops:
  0.6 44.1 %shard_map.165 = (f32[449,128]{1,0:T(8,128)}, f32[449,128]{1,0:T(8,128)}, f32[449,256]{1,0:T(8,128)}, bf16[256,256]{1,0:T(8,128)(2,1)}) custom-call(bf16[512,3584]{1,0:T(8,128)(2,1)} %hid_h.1, bf16[512,128]{1,0:T(8,128)(2,1)} %key_h.1, bf16[512,128]{1,0:T(8,128)(2,1)} %val_h.1, bf16[256,1024]{1,0:T(8,128)(2,1)} %vis_h.1, bf16[256,3584]{1,0:T(8,128)(2,1)} %bitcast.7, ...), custom_call_target="tpu_custom_call" | custom-call | tf_op jit(solution)/shard_map/pallas_call | solution.py:307
  44.8 2.3 %shard_map.166 = (f32[449,128]{1,0:T(8,128)}, f32[449,128]{1,0:T(8,128)}, f32[449,256]{1,0:T(8,128)}, bf16[256,256]{1,0:T(8,128)(2,1)}) custom-call(f32[449,128]{1,0:T(8,128)} %get-tuple-element.12.refs_0_, f32[449,128]{1,0:T(8,128)} %get-tuple-element.13.refs_1_, f32[449,256]{1,0:T(8,128)} %get-tuple-element.14.refs_2_, ...), custom_call_target="tpu_custom_call" | custom-call | tf_op jit(solution)/shard_map/pallas_call | solution.py:350
where the time goes:
time: 47.2 us; the launch traced here: 47 us
  Pallas kernels  46.4 us (98%)
  between operations  0.64 us (1%)
    pallas_call x1, Pallas kernels, per_device(): pl.pallas_call(functools.partial(kernel, (n, mp, shard, rp, spread, cap))...  44.1 us
    pallas_call x1, Pallas kernels, per_device(): pl.pallas_call(finish, out_shape=tuple((jax.ShapeDtypeStruct(x.shape, x.d...  2.26 us

commit v1 on v0

--- a/solution.py
+++ b/solution.py
@@ -34,33 +34,36 @@
     key_o, val_o, proj_o, hand_o,
     hid, key, val, vis, cot, fc1, fc2,
     big_k, big_v, big_c,
-    cot_send, cot_recv,
+    cot_mine, cot_recv,
     k0, k0r, k1, k1r, k2, k2r,
     v0, v0r, v1, v1r, v2, v2r,
-    z_send, z_recv, gath,
+    z_own, z_send, z_recv, pack, hbuf, acc, rs_send, rs_recv,
     load_sem, cot_ss, cot_rs, z_ss, z_rs,
     k0_s, k0_r, k1_s, k1_r, k2_s, k2_r,
     v0_s, v0_r, v1_s, v1_r, v2_s, v2_r,
-    g_s, g_r, f_s, f_r,
+    h_ss, h_rs, p_ss, p_rs,
 ):
-    n, mp, shard, rows_pad, spread, cap = cfg
+    n, mp, shard, rows_pad, spread, cap, nf = cfg
     nc, na, nb = factors(n)
+    chips = n // nc
     me = lax.axis_index("dp")
     col = lax.axis_index("mp")
     dc = lax.rem(me, nc)
     da = lax.rem(lax.div(me, nc), na)
     db = lax.div(me, nc * na)
+    chip = lax.div(me, nc)
     tokens, width = hid.shape
     slots = cot.shape[0]
     kc = key.shape[1]
     fcol = hand_o.shape[1]
+    fw = fcol // nf
 
     def rank(c, a, b):
         return (b * na + a) * nc + c
 
     loads = []
     for i, (src, dst) in enumerate(
-        ((cot_h, cot), (vis_h, vis), (fc1_h, fc1), (fc2_h, fc2), (hid_h, hid), (key_h, key), (val_h, val))
+        ((vis_h, vis), (fc1_h, fc1), (fc2_h, fc2), (key_h, key), (val_h, val), (hid_h, hid), (cot_h, cot))
     ):
         cp = pltpu.make_async_copy(src, dst, load_sem.at[i])
         cp.start()
@@ -71,63 +74,55 @@
     for j in range(1, mp):
         pl.semaphore_signal(barrier, inc=1, device_id={"mp": lax.rem(col + j, mp)}, device_id_type=MESH)
 
-    def remote(src, dst, ss, rs, where):
-        cp = pltpu.make_async_remote_copy(
+    def copy_to(src, dst, ss, rs, where):
+        return pltpu.make_async_remote_copy(
             src_ref=src, dst_ref=dst, send_sem=ss, recv_sem=rs, device_id=where, device_id_type=MESH
         )
+
+    def remote(src, dst, ss, rs, where):
+        cp = copy_to(src, dst, ss, rs, where)
         cp.start()
         return cp
 
     step = 512 if width % 512 == 0 else 128
+    sent = []
 
     loads[0].wait()
-    half = 128
-
-    def turn(i, _):
-        at = pl.multiple_of(i * step, step)
-        for h in range(slots // half):
-            piece = cot[h * half : (h + 1) * half, pl.ds(at, step)].astype(F32)
-            big_c[h, pl.ds(at, step), :] = piece.T
-        return 0
-
-    lax.fori_loop(0, width // step, turn, 0)
-    tail = big_c.shape[1] - width
-    big_c[:, width:, :] = jnp.zeros((slots // half, tail, half), F32)
-    for r in range(n):
-        for h in range(slots // half):
-            cot_send[r, :, h * half : (h + 1) * half] = big_c[h, r * shard : r * shard + rows_pad, :].astype(BF)
-    pl.semaphore_wait(barrier, n - 1 + mp - 1)
-    cot_cps = []
-
-    def send_cot():
-        for j in range(1, n):
-            to = lax.rem(me + j, n)
-            cot_cps.append(remote(cot_send.at[to], cot_recv.at[j - 1], cot_ss.at[j - 1], cot_rs.at[j - 1], {"dp": to}))
-
-    send_cot()
-
-    loads[1].wait()
     values = vis[...].astype(F32)
     center = jnp.mean(values, axis=1, keepdims=True)
     cen = values - center
     var = jnp.mean(cen * cen, axis=1, keepdims=True)
     normed = (cen * lax.rsqrt(var + 1e-06) * gain[...] + beta[...]).astype(BF)
+    loads[1].wait()
+    hidden = erf_gelu(jnp.dot(normed, fc1[...], preferred_element_type=F32) + fc1_b[...]).astype(BF)
     loads[2].wait()
-    hidden = erf_gelu(jnp.dot(normed, fc1[...], preferred_element_type=F32) + fc1_b[...]).astype(BF)
-    loads[3].wait()
-
-    def feat(i):
-        return pl.ds(pl.multiple_of(i * fcol, 128), fcol)
-
-    z_cps = []
+
+    def feat(i, f=0, w=fcol):
+        return pl.ds(pl.multiple_of(i * fcol + f * fw, 128 if fw % 128 == 0 else fw), w)
+
     order = sorted(range(1, mp), key=lambda j: abs(j - mp / 2))
-    for j in order:
-        to = lax.rem(col + j, mp)
-        z_send[j - 1] = jnp.dot(hidden, fc2[:, feat(to)], preferred_element_type=F32).astype(BF)
-        z_cps.append(remote(z_send.at[j - 1], z_recv.at[j - 1], z_ss.at[j - 1], z_rs.at[j - 1], {"mp": to}))
+
+    def z_copy(f, j):
+        return copy_to(
+            z_send.at[f, j - 1], z_recv.at[f, j - 1], z_ss.at[f, j - 1], z_rs.at[f, j - 1],
+            {"mp": lax.rem(col + j, mp)},
+        )
+
+    for i, j in enumerate(order):
+        part = jnp.dot(hidden, fc2[:, feat(lax.rem(col + j, mp))], preferred_element_type=F32).astype(BF)
+        for f in range(nf):
+            z_send[f, j - 1] = part[:, f * fw : (f + 1) * fw]
+        if i == 0:
+            pl.semaphore_wait(barrier, n - 1 + mp - 1)
+        z_copy(0, j).start()
+    for f in range(1, nf):
+        for j in order:
+            z_copy(f, j).start()
     own = jnp.dot(hidden, fc2[:, feat(col)], preferred_element_type=F32)
-
-    for cp in loads[4:]:
+    for f in range(nf):
+        z_own[f] = own[:, f * fw : (f + 1) * fw]
+
+    for cp in loads[3:6]:
         cp.wait()
     kv = jnp.concatenate([key[...], val[...]], axis=1)
 
@@ -139,6 +134,7 @@
         return 0
 
     lax.fori_loop(0, width // step, product, 0)
+    tail = big_k.shape[0] - width
     first = lax.broadcasted_iota(jnp.int32, (tail, kc), 0) == 0
     big_k[width:, :] = jnp.where(first, jnp.sum(key[...].astype(F32), axis=0, keepdims=True), 0.0)
     big_v[width:, :] = jnp.where(first, jnp.sum(val[...].astype(F32), axis=0, keepdims=True), 0.0)
@@ -165,6 +161,39 @@
     at_b = lambda b: rank(dc, da, b)
     s0k = exchange(k0, k0r, k0_s, k0_r, dc, nc, at_c)
     s0v = exchange(v0, v0r, v0_s, v0_r, dc, nc, at_c)
+
+    loads[6].wait()
+    half = 128
+
+    def turn(i, _):
+        at = pl.multiple_of(i * step, step)
+        for h in range(slots // half):
+            piece = cot[h * half : (h + 1) * half, pl.ds(at, step)].astype(F32)
+            big_c[h, pl.ds(at, step), :] = piece.T
+        return 0
+
+    lax.fori_loop(0, width // step, turn, 0)
+    ctail = big_c.shape[1] - width
+    big_c[:, width:, :] = jnp.zeros((slots // half, ctail, half), F32)
+    for r in range(n):
+        for h in range(slots // half):
+            cot_mine[r % nc, r // nc, :, h * half : (h + 1) * half] = big_c[
+                h, r * shard : r * shard + rows_pad, :
+            ].astype(BF)
+    cot_cps = exchange(cot_mine, cot_recv, cot_ss, cot_rs, dc, nc, at_c)
+
+    for cp in s0k:
+        cp.wait_recv()
+    for a in range(na):
+        for b in range(nb):
+            k1[a, b] = added(k0, k0r, dc, nc, (a, b)).astype(BF)
+    s1k = exchange(k1, k1r, k1_s, k1_r, da, na, at_a)
+    for cp in s0v:
+        cp.wait_recv()
+    for b in range(nb):
+        for a in range(na):
+            v1[b, a] = added(v0, v0r, dc, nc, (b, a)).astype(BF)
+    s1v = exchange(v1, v1r, v1_s, v1_r, db, nb, at_b)
 
     rows = vis.shape[0]
     images = counts.shape[1]
@@ -182,38 +211,80 @@
     slot_id = lax.broadcasted_iota(jnp.int32, (spread * cap, rows), 0)
     select = jnp.where(slot_id == target, 1.0, 0.0).astype(BF)
 
-    for cp in s0k:
-        cp.wait_recv()
-    for a in range(na):
-        for b in range(nb):
-            k1[a, b] = added(k0, k0r, dc, nc, (a, b)).astype(BF)
-    s1k = exchange(k1, k1r, k1_s, k1_r, da, na, at_a)
-    for cp in s0v:
-        cp.wait_recv()
-    for b in range(nb):
-        for a in range(na):
-            v1[b, a] = added(v0, v0r, dc, nc, (b, a)).astype(BF)
-    s1v = exchange(v1, v1r, v1_s, v1_r, db, nb, at_b)
-
-    for cp in z_cps:
-        cp.wait_recv()
-    summed = own
-    for j in range(1, mp):
-        summed = summed + z_recv[j - 1].astype(F32)
-    encoded = (
-        vis[:, feat(col)].astype(F32) + scale[:, feat(col)] * (summed + fc2_b[:, feat(col)])
-    ).astype(BF)
-    gath[me] = jnp.dot(select, encoded, preferred_element_type=F32).astype(BF)
-    chips = n // nc
-    chip = lax.div(me, nc)
-    g_cps, f_cps = [], []
-    for j in range(1, nc):
-        f_cps.append(
-            remote(gath.at[me], gath.at[me], f_s.at[0, j - 1], f_r.at[0, j - 1], {"dp": at_c(lax.rem(dc + j, nc))})
+    def hand_copy(f, k, t):
+        to = lax.rem(me + k, n)
+        inside = lax.rem(to, nc)
+        return copy_to(
+            pack.at[f, k - 1], hbuf.at[f, inside, k - 1], h_ss.at[f, k - 1, t], h_rs.at[f, inside, k - 1],
+            {"dp": lax.div(to, nc) * nc + t},
         )
-    for j in range(1, chips):
-        to = lax.rem(chip + j, chips) * nc + dc
-        g_cps.append(remote(gath.at[me], gath.at[me], g_s.at[j - 1], g_r.at[j - 1], {"dp": to}))
+
+    def each_hand(f, act):
+        for k in range(spread, 0, -1):
+            for t in range(nc):
+                if k < nc:
+                    @pl.when(jnp.logical_not((dc + k < nc) & (dc == t)))
+                    def _():
+                        act(hand_copy(f, k, t))
+                else:
+                    act(hand_copy(f, k, t))
+
+    def encode(f):
+        for j in range(1, mp):
+            z_copy(f, j).wait_recv()
+        summed = z_own[f]
+        for j in range(1, mp):
+            summed = summed + z_recv[f, j - 1].astype(F32)
+        at = feat(col, f, fw)
+        encoded = (vis[:, at].astype(F32) + scale[:, at] * (summed + fc2_b[:, at])).astype(BF)
+        packed = jnp.dot(select, encoded, preferred_element_type=F32).astype(BF)
+        for k in range(1, spread + 1):
+            pack[f, k - 1] = packed[(k - 1) * cap : k * cap, :]
+        for k in range(1, nc):
+            for c in range(nc - k):
+                @pl.when(dc == c)
+                def _():
+                    hbuf[f, c + k, k - 1] = packed[(k - 1) * cap : k * cap, :]
+        each_hand(f, lambda cp: cp.start())
+
+    def hand_wait(f):
+        for k in range(spread, 0, -1):
+            for inside in range(nc):
+                cp = copy_to(
+                    pack.at[f, k - 1], hbuf.at[f, inside, k - 1], h_ss.at[f, k - 1, 0],
+                    h_rs.at[f, inside, k - 1], {"dp": lax.rem(me + k, n)},
+                )
+                if inside >= k:
+                    @pl.when(dc != inside - k)
+                    def _():
+                        cp.wait_recv()
+                else:
+                    cp.wait_recv()
+
+    offs = [(ja, jb) for jb in range(nb) for ja in range(na) if ja or jb]
+    offs.sort(key=lambda o: -((o[0] > 0) + (o[1] > 0)))
+
+    def rs_copy(f, i):
+        ja, jb = offs[i]
+        to = rank(dc, lax.rem(da + ja, na), lax.rem(db + jb, nb))
+        return copy_to(rs_send.at[f, i], rs_recv.at[f, i], p_ss.at[f, i], p_rs.at[f, i], {"dp": to})
+
+    def product_of(f, to):
+        got = hbuf[f, dc].reshape(slots, fw)
+        total = jnp.dot(cot_mine[dc, to], got, preferred_element_type=F32)
+        for j in range(1, nc):
+            other = hbuf[f, lax.rem(dc + nc - j, nc)].reshape(slots, fw)
+            total = total + jnp.dot(cot_recv[j - 1, to], other, preferred_element_type=F32)
+        return total
+
+    def project(f):
+        for i, (ja, jb) in enumerate(offs):
+            to = lax.rem(db + jb, nb) * na + lax.rem(da + ja, na)
+            rs_send[f, i] = product_of(f, to).astype(BF)
+            rs_copy(f, i).start()
+        acc[f] = product_of(f, chip)
+
+    encode(0)
 
     for cp in s1k:
         cp.wait_recv()
@@ -226,43 +297,37 @@
         v2[a] = added(v1, v1r, db, nb, (a,)).astype(BF)
     s2v = exchange(v2, v2r, v2_s, v2_r, da, na, at_a)
 
-    for j in range(1, chips):
-        g_cps[j - 1].wait_recv()
-        source = lax.rem(chip + chips - j, chips) * nc + dc
-        for i in range(1, nc):
-            f_cps.append(
-                remote(
-                    gath.at[source], gath.at[source], f_s.at[j, i - 1], f_r.at[j, i - 1],
-                    {"dp": at_c(lax.rem(dc + i, nc))},
-                )
-            )
-    for cp in f_cps:
-        cp.wait_recv()
-
-    def received(r):
-        parts = []
-        for k in range(1, spread + 1):
-            source = lax.rem(r + n - k, n)
-            parts.append(gath[source, (k - 1) * cap : k * cap, :])
-        return jnp.concatenate(parts, axis=0)
-
-    mine = received(me)
-    hand_o[...] = mine
-    total = jnp.dot(cot_send[me], mine, preferred_element_type=F32)
-    for j in range(1, n):
-        cot_cps[j - 1].wait_recv()
-        total = total + jnp.dot(
-            cot_recv[j - 1], received(lax.rem(me + n - j, n)), preferred_element_type=F32
-        )
-    proj_o[...] = total[:shard]
-
+    for cp in cot_cps:
+        cp.wait_recv()
+    hand_wait(0)
+    project(0)
+    for f in range(1, nf):
+        encode(f)
+        hand_wait(f)
+        project(f)
+
+    for f in range(nf):
+        hand_o[:, f * fw : (f + 1) * fw] = hbuf[f, dc].reshape(slots, fw)
     for cp in s2k:
         cp.wait_recv()
     key_o[...] = added(k2, k2r, db, nb, ())[:shard]
     for cp in s2v:
         cp.wait_recv()
     val_o[...] = added(v2, v2r, da, na, ())[:shard]
-    for cp in cot_cps + z_cps + s0k + s0v + s1k + s1v + s2k + s2v + g_cps + f_cps:
+    for f in range(nf):
+        total = acc[f]
+        for i in range(len(offs)):
+            rs_copy(f, i).wait_recv()
+            total = total + rs_recv[f, i].astype(F32)
+        proj_o[:, f * fw : (f + 1) * fw] = total[:shard]
+
+    for f in range(nf):
+        for j in range(1, mp):
+            z_copy(f, j).wait_send()
+        each_hand(f, lambda cp: cp.wait_send())
+        for i in range(len(offs)):
+            rs_copy(f, i).wait_send()
+    for cp in cot_cps + s0k + s0v + s1k + s1v + s2k + s2v:
         cp.wait_send()
 
 
@@ -285,6 +350,8 @@
     kc = key_grad.shape[1]
     rows, feats = visual_rows.shape
     fcol = feats // mp
+    nf = max(1, fcol // 128)
+    fw = fcol // nf
     tall = up(max((n - 1) * shard + rp, width + 8), 8)
     any_spec = pl.BlockSpec(memory_space=pl.ANY)
     vm = pl.BlockSpec(memory_space=pltpu.VMEM)
@@ -305,7 +372,7 @@
         return [dma(q - 1) for q in (nc, nc, q1, q1, q2, q2)]
 
     outs = pl.pallas_call(
-        functools.partial(kernel, (n, mp, shard, rp, spread, cap)),
+        functools.partial(kernel, (n, mp, shard, rp, spread, cap, nf)),
         out_shape=(
             jax.ShapeDtypeStruct((shard, kc), F32),
             jax.ShapeDtypeStruct((shard, kc), F32),
@@ -325,20 +392,28 @@
             pltpu.VMEM((tall, kc), F32),
             pltpu.VMEM((tall, kc), F32),
             pltpu.VMEM((slots // 128, tall, 128), F32),
-            pltpu.VMEM((n, rp, slots), BF),
-            pltpu.VMEM((n - 1, rp, slots), BF),
+            pltpu.VMEM((nc, n // nc, rp, slots), BF),
+            pltpu.VMEM((max(nc - 1, 1), n // nc, rp, slots), BF),
         ]
         + stages(na, nb)
         + stages(nb, na)
         + [
-            pltpu.VMEM((mp - 1, rows, fcol), BF),
-            pltpu.VMEM((mp - 1, rows, fcol), BF),
-            pltpu.VMEM((n, slots, fcol), BF),
-            dma(7), dma(n - 1), dma(n - 1), dma(mp - 1), dma(mp - 1),
+            pltpu.VMEM((nf, rows, fw), F32),
+            pltpu.VMEM((nf, mp - 1, rows, fw), BF),
+            pltpu.VMEM((nf, mp - 1, rows, fw), BF),
+            pltpu.VMEM((nf, spread, cap, fw), BF),
+            pltpu.VMEM((nf, nc, spread, cap, fw), BF),
+            pltpu.VMEM((nf, rp, fw), F32),
+            pltpu.VMEM((nf, n // nc - 1, rp, fw), BF),
+            pltpu.VMEM((nf, n // nc - 1, rp, fw), BF),
+            dma(7), dma(nc - 1), dma(nc - 1), dma(nf, mp - 1), dma(nf, mp - 1),
         ]
         + stage_sems(na, nb)
         + stage_sems(nb, na)
-        + [dma(n // nc - 1), dma(n // nc - 1), dma(n // nc, nc - 1), dma(n // nc, nc - 1)],
+        + [
+            dma(nf, spread, nc), dma(nf, nc, spread),
+            dma(nf, n // nc - 1), dma(nf, n // nc - 1),
+        ],
         compiler_params=pltpu.CompilerParams(
             collective_id=0, has_side_effects=True, vmem_limit_bytes=60 * 1024 * 1024
         ),

time: 47.2 us -> 43.5 us (0.922)
  the two profiles are of different devices: /device:TPU:1 before, /device:TPU:0 now
where the time goes in v1:
time: 43.5 us; the launch traced here: 43.3 us
  Pallas kernels  42.7 us (98%)
  between operations  0.64 us (1%)
    pallas_call x1, Pallas kernels, per_device(): pl.pallas_call(functools.partial(kernel, (n, mp, shard, rp, spread, cap,...  40.4 us
    pallas_call x1, Pallas kernels, per_device(): pl.pallas_call(finish, out_shape=tuple((jax.ShapeDtypeStruct(x.shape, x.d...  2.26 us

profile of v1, /device:TPU:0, one launch (start us, length us, event | category | flops | bytes accessed | tf_op | source)
XLA Modules:
  0.0 43.3 jit_solution(13353050999263448277)
XLA Ops:
  0.6 40.4 %shard_map.165 = (f32[449,128]{1,0:T(8,128)}, f32[449,128]{1,0:T(8,128)}, f32[449,256]{1,0:T(8,128)}, bf16[256,256]{1,0:T(8,128)(2,1)}) custom-call(bf16[512,3584]{1,0:T(8,128)(2,1)} %hid_h.1, bf16[512,128]{1,0:T(8,128)(2,1)} %key_h.1, bf16[512,128]{1,0:T(8,128)(2,1)} %val_h.1, bf16[256,1024]{1,0:T(8,128)(2,1)} %vis_h.1, bf16[256,3584]{1,0:T(8,128)(2,1)} %bitcast.7, ...), custom_call_target="tpu_custom_call" | custom-call | tf_op jit(solution)/shard_map/pallas_call | solution.py:374
  41.1 2.3 %shard_map.166 = (f32[449,128]{1,0:T(8,128)}, f32[449,128]{1,0:T(8,128)}, f32[449,256]{1,0:T(8,128)}, bf16[256,256]{1,0:T(8,128)(2,1)}) custom-call(f32[449,128]{1,0:T(8,128)} %get-tuple-element.12.refs_0_, f32[449,128]{1,0:T(8,128)} %get-tuple-element.13.refs_1_, f32[449,256]{1,0:T(8,128)} %get-tuple-element.14.refs_2_, ...), custom_call_target="tpu_custom_call" | custom-call | tf_op jit(solution)/shard_map/pallas_call | solution.py:425

commit v2 on v1

v2 whole, which is shorter than its diff:
```python
import functools

import jax
import jax.numpy as jnp
from jax import lax
from jax.experimental import pallas as pl
from jax.experimental.pallas import tpu as pltpu
from jax.sharding import PartitionSpec as P

MESH = pl.DeviceIdType.MESH
BF = jnp.bfloat16
F32 = jnp.float32


def up(x, m):
    return -(-x // m) * m


def factors(n):
    core = 2 if n % 2 == 0 else 1
    rest = n // core
    inner = max(f for f in range(1, rest + 1) if rest % f == 0 and f * f <= rest)
    return core, inner, rest // inner


def erf_gelu(x):
    return 0.5 * x * (1.0 + lax.erf(x * (0.5**0.5)))


def kernel(
    cfg,
    hid_h, key_h, val_h, vis_h, cot_h, fc1_h, fc2_h,
    gain_h, beta_h, fc1_bh, fc2_bh, scale_h, counts_h, offsets_h,
    key_o, val_o, proj_o, hand_o,
    hid, key, val, vis, cot, fc1, fc2,
    gain, beta, fc1_b, fc2_b, scale, counts, offsets,
    big_k, big_v, big_c,
    cot_mine, cot_recv,
    k0, k0r, k1, k1r, k2, k2r,
    v0, v0r, v1, v1r, v2, v2r,
    z_full, z_own, z_send, z_recv, z_relay, pack, hbuf, acc, rs_send, rs_recv,
    x1, x1r, x2, x2r, y1, y1r, y2, y2r,
    load_sem, cot_ss, cot_rs, z_ss, z_rs, e_ss, e_rs,
    k0_s, k0_r, k1_s, k1_r, k2_s, k2_r,
    v0_s, v0_r, v1_s, v1_r, v2_s, v2_r,
    h_ss, h_rs, g_ss, g_rs, p_ss, p_rs,
    x1_s, x1_r, x2_s, x2_r, y1_s, y1_r, y2_s, y2_r,
):
    n, mp, shard, rows_pad, spread, cap, nf, groups = cfg
    nc, na, nb = factors(n)
    chips = n // nc
    me = lax.axis_index("dp")
    col = lax.axis_index("mp")
    dc = lax.rem(me, nc)
    da = lax.rem(lax.div(me, nc), na)
    db = lax.div(me, nc * na)
    chip = lax.div(me, nc)
    tokens, width = hid.shape
    slots = cot.shape[0]
    kc = key.shape[1]
    fcol = hand_o.shape[1]
    fw = fcol // nf

    def rank(c, a, b):
        return (b * na + a) * nc + c

    loads = []
    for i, (src, dst) in enumerate(
        (
            (vis_h, vis), (gain_h, gain), (beta_h, beta), (fc1_h, fc1), (fc1_bh, fc1_b), (fc2_h, fc2),
            (key_h, key), (val_h, val), (hid_h, hid), (cot_h, cot),
            (fc2_bh, fc2_b), (scale_h, scale), (counts_h, counts), (offsets_h, offsets),
        )
    ):
        cp = pltpu.make_async_copy(src, dst, load_sem.at[i])
        cp.start()
        loads.append(cp)
    barrier = pltpu.get_barrier_semaphore()
    for j in range(1, n):
        pl.semaphore_signal(barrier, inc=1, device_id={"dp": lax.rem(me + j, n)}, device_id_type=MESH)
    for j in range(1, mp):
        pl.semaphore_signal(barrier, inc=1, device_id={"mp": lax.rem(col + j, mp)}, device_id_type=MESH)

    def copy_to(src, dst, ss, rs, where):
        return pltpu.make_async_remote_copy(
            src_ref=src, dst_ref=dst, send_sem=ss, recv_sem=rs, device_id=where, device_id_type=MESH
        )

    def remote(src, dst, ss, rs, where):
        cp = copy_to(src, dst, ss, rs, where)
        cp.start()
        return cp

    loads[0].wait()
    values = vis[...].astype(F32)
    center = jnp.mean(values, axis=1, keepdims=True)
    cen = values - center
    var = jnp.mean(cen * cen, axis=1, keepdims=True)
    for cp in loads[1:3]:
        cp.wait()
    normed = (cen * lax.rsqrt(var + 1e-06) * gain[...] + beta[...]).astype(BF)
    for cp in loads[3:5]:
        cp.wait()
    hidden = erf_gelu(jnp.dot(normed, fc1[...], preferred_element_type=F32) + fc1_b[...]).astype(BF)
    loads[5].wait()
    partial = jnp.dot(hidden, fc2[...], preferred_element_type=F32)
    for m in range(mp):
        for f in range(nf):
            piece = partial[:, m * fcol + f * fw : m * fcol + (f + 1) * fw]
            z_full[f, m] = piece
            z_send[f, m] = piece.astype(BF)

    def feat(i, f=0, w=fcol):
        return pl.ds(pl.multiple_of(i * fcol + f * fw, 128 if fw % 128 == 0 else fw), w)

    chain = mp >= 4
    low, high = col == 0, col == mp - 1
    if chain:
        edge = low | high
        near = jnp.where(low, 1, mp - 2)
        inner = (col == 1) | (col == mp - 2)
        beyond = jnp.where(col == 1, mp - 1, 0)
        opposite = jnp.where(low, mp - 1, 0)
    order = sorted(range(1, mp), key=lambda j: abs(j - mp / 2))

    def z_copy(f, j):
        to = lax.rem(col + j, mp)
        return copy_to(z_send.at[f, to], z_recv.at[f, j - 1], z_ss.at[f, j - 1], z_rs.at[f, j - 1], {"mp": to})

    def e_copy(f):
        return copy_to(z_send.at[f, opposite], z_relay.at[f], e_ss.at[f], e_rs.at[f], {"mp": near})

    def r_copy(f):
        j = jnp.where(col == 1, mp - 2, 2)
        return copy_to(z_send.at[f, beyond], z_recv.at[f, j - 1], z_ss.at[f, j - 1], z_rs.at[f, j - 1], {"mp": beyond})

    def held(j):
        to = lax.rem(col + j, mp)
        return (low & (to == mp - 1)) | (high & (to == 0)), ((col == 1) & (to == mp - 1)) | ((col == mp - 2) & (to == 0))

    def z_start(f):
        for j in order:
            if chain:
                skip, later = held(j)

                @pl.when(jnp.logical_not(skip | later))
                def _():
                    z_copy(f, j).start()
            else:
                z_copy(f, j).start()

    def z_pass(f):
        if chain:
            @pl.when(inner)
            def _():
                e_copy(f).wait_recv()
                z_send[f, beyond] = (z_full[f, beyond] + z_relay[f].astype(F32)).astype(BF)
                r_copy(f).start()

    def z_sum(f):
        z_own[f] = z_full[f, col]
        for j in order:
            def take():
                z_copy(f, j).wait_recv()
                z_own[f] += z_recv[f, j - 1].astype(F32)

            source = lax.rem(col + mp - j, mp)
            if chain:
                @pl.when(jnp.logical_not((low & (source == mp - 1)) | (high & (source == 0))))
                def _():
                    take()
            else:
                take()

    def z_drain(f):
        if chain:
            @pl.when(edge)
            def _():
                e_copy(f).wait_send()
        for j in order:
            if chain:
                skip, _ = held(j)

                @pl.when(jnp.logical_not(skip))
                def _():
                    z_copy(f, j).wait_send()
            else:
                z_copy(f, j).wait_send()

    pl.semaphore_wait(barrier, n - 1 + mp - 1)
    if chain:
        @pl.when(edge)
        def _():
            for f in range(nf):
                e_copy(f).start()
    for f in range(nf):
        z_start(f)

    for cp in loads[6:9]:
        cp.wait()
    kv = jnp.concatenate([key[...], val[...]], axis=1)
    tail = big_k.shape[0] - width
    first = lax.broadcasted_iota(jnp.int32, (tail, kc), 0) == 0
    big_k[width:, :] = jnp.where(first, jnp.sum(key[...].astype(F32), axis=0, keepdims=True), 0.0)
    big_v[width:, :] = jnp.where(first, jnp.sum(val[...].astype(F32), axis=0, keepdims=True), 0.0)
    nbg = nb // groups
    at_c = lambda c: rank(c, da, db)
    at_a = lambda a: rank(dc, a, db)
    at_b = lambda b: rank(dc, da, b)

    def kv_first(buf, got, ss, rs, g):
        part = pl.ds(g * nbg, nbg)
        cps = []
        for j in range(1, nc):
            to = lax.rem(dc + j, nc)
            cps.append(copy_to(buf.at[to, part], got.at[j - 1, part], ss.at[j - 1, g], rs.at[j - 1, g], {"dp": at_c(to)}))
        return cps

    block = width if groups == 1 else min(width, up((nbg * na * nc - 1) * shard + rows_pad, 128))
    stride = 0 if groups == 1 else (width - block) // (groups - 1)

    def product(i, _):
        at = pl.multiple_of(i * stride, 128)
        res = lax.dot_general(
            hid[:, pl.ds(at, block)], kv, (((0,), (0,)), ((), ())), preferred_element_type=F32
        )
        big_k[pl.ds(at, block), :] = res[:, :kc]
        big_v[pl.ds(at, block), :] = res[:, kc:]
        for g in range(groups):
            @pl.when(i == g)
            def _():
                for b in range(g * nbg, (g + 1) * nbg):
                    for a in range(na):
                        for c in range(nc):
                            r = rank(c, a, b)
                            k0[c, b, a] = big_k[r * shard : r * shard + rows_pad, :].astype(BF)
                            v0[c, b, a] = big_v[r * shard : r * shard + rows_pad, :].astype(BF)
                for cp in kv_first(k0, k0r, k0_s, k0_r, g) + kv_first(v0, v0r, v0_s, v0_r, g):
                    cp.start()
        return 0

    lax.fori_loop(0, groups, product, 0)

    def exchange(buf, got, ss, rs, digit, q, peer_of):
        cps = []
        for j in range(1, q):
            to = lax.rem(digit + j, q)
            cps.append(copy_to(buf.at[to], got.at[j - 1], ss.at[j - 1], rs.at[j - 1], {"dp": peer_of(to)}))
        return cps

    def begin(cps):
        for cp in cps:
            cp.start()
        return cps

    def added(buf, got, digit, q, at):
        total = buf[(digit,) + at].astype(F32)
        for j in range(1, q):
            total = total + got[(j - 1,) + at].astype(F32)
        return total

    loads[9].wait()
    half = 128
    step = width // 2 if width % 256 == 0 else 128

    def turn(i, _):
        at = pl.multiple_of(i * step, 128)
        for h in range(slots // half):
            piece = cot[h * half : (h + 1) * half, pl.ds(at, step)].astype(F32)
            big_c[h, pl.ds(at, step), :] = piece.T
        return 0

    lax.fori_loop(0, width // step, turn, 0)

    def kv_second(g):
        for b in range(g * nbg, (g + 1) * nbg):
            for a in range(na):
                k1[a, b] = added(k0, k0r, dc, nc, (b, a)).astype(BF)
                v1[b, a] = added(v0, v0r, dc, nc, (b, a)).astype(BF)
        part = pl.ds(g * nbg, nbg)
        for j in range(1, na):
            k1_copy(j, g).start()
        for j in range(1, nb):
            @pl.when(lax.div(lax.rem(db + j, nb), nbg) == g)
            def _():
                v1_copy(j).start()

    def k1_copy(j, g):
        part = pl.ds(g * nbg, nbg)
        to = lax.rem(da + j, na)
        return copy_to(k1.at[to, part], k1r.at[j - 1, part], k1_s.at[j - 1, g], k1_r.at[j - 1, g], {"dp": at_a(to)})

    def v1_copy(j):
        to = lax.rem(db + j, nb)
        return copy_to(v1.at[to], v1r.at[j - 1], v1_s.at[j - 1], v1_r.at[j - 1], {"dp": at_b(to)})

    for g in range(groups):
        for cp in kv_first(k0, k0r, k0_s, k0_r, g) + kv_first(v0, v0r, v0_s, v0_r, g):
            cp.wait_recv()
        kv_second(g)
        if g == 0:
            z_pass(0)

    ctail = big_c.shape[1] - width
    big_c[:, width:, :] = jnp.zeros((slots // half, ctail, half), F32)
    for r in range(n):
        for h in range(slots // half):
            cot_mine[r % nc, r // nc, :, h * half : (h + 1) * half] = big_c[
                h, r * shard : r * shard + rows_pad, :
            ].astype(BF)
    cot_cps = begin(exchange(cot_mine, cot_recv, cot_ss, cot_rs, dc, nc, at_c))

    for cp in loads[10:]:
        cp.wait()
    rows = vis.shape[0]
    images = counts.shape[1]
    place = lax.broadcasted_iota(jnp.int32, (1, rows), 1)
    target = jnp.full((1, rows), -1, jnp.int32)
    start = jnp.int32(0)
    for i in range(images):
        cnt, off = counts[0, i], offsets[0, i]
        before = jnp.int32(0)
        for e in range(i):
            before = before + jnp.where(offsets[0, e] == off, counts[0, e], 0)
        inside = (place >= start) & (place < start + cnt)
        target = jnp.where(inside, (off - 1) * cap + before + place - start, target)
        start = start + cnt
    slot_id = lax.broadcasted_iota(jnp.int32, (spread * cap, rows), 0)
    select = jnp.where(slot_id == target, 1.0, 0.0).astype(BF)

    def hand_copy(f, k):
        to = lax.rem(me + k, n)
        inside = lax.rem(to, nc)
        return copy_to(pack.at[f, k - 1], hbuf.at[f, inside, k - 1], h_ss.at[f, k - 1], h_rs.at[f, k - 1], {"dp": to})

    def share_copy(f, k, j):
        to = lax.rem(dc + j, nc)
        block = hbuf.at[f, dc, k - 1]
        return copy_to(block, block, g_ss.at[f, k - 1, j - 1], g_rs.at[f, k - 1, j - 1], {"dp": at_c(to)})

    def encode(f):
        z_sum(f)
        at = feat(col, f, fw)
        encoded = (vis[:, at].astype(F32) + scale[:, at] * (z_own[f] + fc2_b[:, at])).astype(BF)
        packed = jnp.dot(select, encoded, preferred_element_type=F32).astype(BF)
        for k in range(1, spread + 1):
            pack[f, k - 1] = packed[(k - 1) * cap : k * cap, :]
        for k in range(spread, 0, -1):
            hand_copy(f, k).start()

    def hand_wait(f):
        for k in range(1, spread + 1):
            hand_copy(f, k).wait_recv()
            for j in range(1, nc):
                share_copy(f, k, j).start()
        for k in range(1, spread + 1):
            for j in range(1, nc):
                share_copy(f, k, j).wait_recv()

    offs = [(ja, jb) for jb in range(nb) for ja in range(na) if ja or jb]
    offs.sort(key=lambda o: -((o[0] > 0) + (o[1] > 0)))

    def rs_copy(i):
        ja, jb = offs[i]
        to = lax.rem(db + jb, nb) * na + lax.rem(da + ja, na)
        return copy_to(rs_send.at[to], rs_recv.at[i], p_ss.at[i], p_rs.at[i], {"dp": to * nc + dc})

    def product_of(f, to):
        got = hbuf[f, dc].reshape(slots, fw)
        total = jnp.dot(cot_mine[dc, to], got, preferred_element_type=F32)
        for j in range(1, nc):
            other = hbuf[f, lax.rem(dc + nc - j, nc)].reshape(slots, fw)
            total = total + jnp.dot(cot_recv[j - 1, to], other, preferred_element_type=F32)
        return total

    top = x1.shape[-2]

    def staged(f):
        for a in range(na):
            for b in range(nb):
                total = product_of(f, b * na + a).astype(BF)
                x1[f, a, b] = total[:top]
                y1[f, b, a] = total[top:]
        return begin(x_first(f) + y_first(f))

    def x_first(f):
        return exchange(x1.at[f], x1r.at[f], x1_s.at[f], x1_r.at[f], da, na, at_a)

    def y_first(f):
        return exchange(y1.at[f], y1r.at[f], y1_s.at[f], y1_r.at[f], db, nb, at_b)

    def x_second(f):
        return exchange(x2.at[f], x2r.at[f], x2_s.at[f], x2_r.at[f], db, nb, at_b)

    def y_second(f):
        return exchange(y2.at[f], y2r.at[f], y2_s.at[f], y2_r.at[f], da, na, at_a)

    def staged_next(f):
        for cp in x_first(f):
            cp.wait_recv()
        for b in range(nb):
            x2[f, b] = added(x1.at[f], x1r.at[f], da, na, (b,)).astype(BF)
        begin(x_second(f))
        for cp in y_first(f):
            cp.wait_recv()
        for a in range(na):
            y2[f, a] = added(y1.at[f], y1r.at[f], db, nb, (a,)).astype(BF)
        begin(y_second(f))

    def direct(f):
        for to in range(chips):
            total = product_of(f, to)
            acc[to] = total
            rs_send[to] = total.astype(BF)
        for i in range(len(offs)):
            rs_copy(i).start()

    for f in range(1, nf):
        z_pass(f)
    for f in range(nf):
        encode(f)

    for g in range(groups):
        for j in range(1, na):
            k1_copy(j, g).wait_recv()
    for b in range(nb):
        k2[b] = added(k1, k1r, da, na, (b,)).astype(BF)
    s2k = begin(exchange(k2, k2r, k2_s, k2_r, db, nb, at_b))
    for j in range(1, nb):
        v1_copy(j).wait_recv()
    for a in range(na):
        v2[a] = added(v1, v1r, db, nb, (a,)).astype(BF)
    s2v = begin(exchange(v2, v2r, v2_s, v2_r, da, na, at_a))

    for cp in cot_cps:
        cp.wait_recv()
    for f in range(nf - 1):
        hand_wait(f)
        staged(f)
    hand_wait(nf - 1)
    direct(nf - 1)
    for f in range(nf - 1):
        staged_next(f)

    for f in range(nf):
        hand_o[:, f * fw : (f + 1) * fw] = hbuf[f, dc].reshape(slots, fw)
    for cp in s2k:
        cp.wait_recv()
    key_o[...] = added(k2, k2r, db, nb, ())[:shard]
    for cp in s2v:
        cp.wait_recv()
    val_o[...] = added(v2, v2r, da, na, ())[:shard]
    total = acc[chip]
    for i in range(len(offs)):
        rs_copy(i).wait_recv()
        total = total + rs_recv[i].astype(F32)
    proj_o[:, (nf - 1) * fw :] = total[:shard]
    for f in range(nf - 1):
        for cp in x_second(f):
            cp.wait_recv()
        proj_o[:top, f * fw : (f + 1) * fw] = added(x2.at[f], x2r.at[f], db, nb, ())
        for cp in y_second(f):
            cp.wait_recv()
        proj_o[top:, f * fw : (f + 1) * fw] = added(y2.at[f], y2r.at[f], da, na, ())[: shard - top]

    for f in range(nf):
        z_drain(f)
        for k in range(1, spread + 1):
            hand_copy(f, k).wait_send()
            for j in range(1, nc):
                share_copy(f, k, j).wait_send()
    for f in range(nf - 1):
        for cp in x_first(f) + y_first(f) + x_second(f) + y_second(f):
            cp.wait_send()
    for i in range(len(offs)):
        rs_copy(i).wait_send()
    for g in range(groups):
        for cp in kv_first(k0, k0r, k0_s, k0_r, g) + kv_first(v0, v0r, v0_s, v0_r, g):
            cp.wait_send()
        for j in range(1, na):
            k1_copy(j, g).wait_send()
    for j in range(1, nb):
        v1_copy(j).wait_send()
    for cp in cot_cps + s2k + s2v:
        cp.wait_send()


def finish(*refs):
    half = len(refs) // 2
    sems = refs[-1]
    cps = []
    for i, (src, dst) in enumerate(zip(refs[:half], refs[half:-1])):
        cp = pltpu.make_async_copy(src, dst, sems.at[i])
        cp.start()
        cps.append(cp)
    for cp in cps:
        cp.wait()


def per_device(
    n, mp, hidden_rows, key_grad, value_grad, visual_rows, visual_cotangent, norm_gain, norm_bias,
    fc1_weight, fc1_bias, fc2_weight, fc2_bias, layer_scale, token_counts, dest_offsets,
):
    tokens, width = hidden_rows.shape
    spread, cap = visual_cotangent.shape[1:3]
    slots = spread * cap
    shard = (width + n) // n
    rp = up(shard, 16)
    nc, na, nb = factors(n)
    chips = n // nc
    kc = key_grad.shape[1]
    rows, feats = visual_rows.shape
    fcol = feats // mp
    nf = max(1, fcol // 128)
    fw = fcol // nf
    groups = 2 if nb % 2 == 0 else 1
    tall = up(max((n - 1) * shard + rp, width + 8), 8)
    top = max(up(rp // 2, 16), 16)
    low = max(rp - top, 16)
    ns = max(nf - 1, 1)
    any_spec = pl.BlockSpec(memory_space=pl.ANY)
    vm = pl.BlockSpec(memory_space=pltpu.VMEM)
    dma = lambda *s: pltpu.SemaphoreType.DMA(tuple(max(x, 1) for x in s))
    bf = lambda *s: pltpu.VMEM(tuple(max(x, 1) for x in s), BF)

    def stages(q1, q2):
        return [
            bf(nc, nb, na, rp, kc), bf(nc - 1, nb, na, rp, kc),
            bf(q1, q2, rp, kc), bf(q1 - 1, q2, rp, kc),
            bf(q2, rp, kc), bf(q2 - 1, rp, kc),
        ]

    def halves(q1, q2, h):
        return [bf(ns, q1, q2, h, fw), bf(ns, q1 - 1, q2, h, fw), bf(ns, q2, h, fw), bf(ns, q2 - 1, h, fw)]

    small = (norm_gain, norm_bias, fc1_bias, fc2_bias, layer_scale)
    outs = pl.pallas_call(
        functools.partial(kernel, (n, mp, shard, rp, spread, cap, nf, groups)),
        out_shape=(
            pltpu.VMEM((shard, kc), F32),
            pltpu.VMEM((shard, kc), F32),
            pltpu.VMEM((shard, fcol), F32),
            pltpu.VMEM((slots, fcol), BF),
        ),
        in_specs=[any_spec] * 14,
        out_specs=(vm, vm, vm, vm),
        scratch_shapes=[
            pltpu.VMEM(x.shape, BF)
            for x in (hidden_rows, key_grad, value_grad, visual_rows)
        ]
        + [bf(slots, width), bf(*fc1_weight.shape), bf(*fc2_weight.shape)]
        + [pltpu.VMEM((1, x.shape[0]), F32) for x in small]
        + [pltpu.SMEM(token_counts.shape, jnp.int32), pltpu.SMEM(dest_offsets.shape, jnp.int32)]
        + [
            pltpu.VMEM((tall, kc), F32),
            pltpu.VMEM((tall, kc), F32),
            pltpu.VMEM((slots // 128, tall, 128), F32),
            bf(nc, chips, rp, slots),
            bf(nc - 1, chips, rp, slots),
        ]
        + stages(na, nb)
        + stages(nb, na)
        + [
            pltpu.VMEM((nf, mp, rows, fw), F32),
            pltpu.VMEM((nf, rows, fw), F32),
            bf(nf, mp, rows, fw),
            bf(nf, mp - 1, rows, fw),
            bf(nf, rows, fw),
            bf(nf, spread, cap, fw),
            bf(nf, nc, spread, cap, fw),
            pltpu.VMEM((chips, rp, fw), F32),
            bf(chips, rp, fw),
            bf(chips - 1, rp, fw),
        ]
        + halves(na, nb, top)
        + halves(nb, na, low)
        + [dma(14), dma(nc - 1), dma(nc - 1), dma(nf, mp - 1), dma(nf, mp - 1), dma(nf), dma(nf)]
        + [dma(nc - 1, groups), dma(nc - 1, groups), dma(na - 1, groups), dma(na - 1, groups), dma(nb - 1), dma(nb - 1)]
        + [dma(nc - 1, groups), dma(nc - 1, groups), dma(nb - 1), dma(nb - 1), dma(na - 1), dma(na - 1)]
        + [dma(nf, spread), dma(nf, spread), dma(nf, spread, nc - 1), dma(nf, spread, nc - 1)]
        + [dma(chips - 1), dma(chips - 1)]
        + [dma(ns, q) for q in (na - 1, na - 1, nb - 1, nb - 1)]
        + [dma(ns, q) for q in (nb - 1, nb - 1, na - 1, na - 1)],
        compiler_params=pltpu.CompilerParams(
            collective_id=0, has_side_effects=True, vmem_limit_bytes=56 * 1024 * 1024
        ),
    )(
        hidden_rows, key_grad, value_grad, visual_rows, visual_cotangent.reshape(slots, width),
        fc1_weight, fc2_weight, *(x[None] for x in small), token_counts, dest_offsets,
    )
    outs = pl.pallas_call(
        finish,
        out_shape=tuple(jax.ShapeDtypeStruct(x.shape, x.dtype) for x in outs),
        in_specs=[vm] * 4,
        out_specs=(any_spec,) * 4,
        scratch_shapes=[dma(4)],
    )(*(pltpu.with_memory_space_constraint(x, pltpu.VMEM) for x in outs))
    return outs[0], outs[1], outs[2], outs[3].reshape(1, spread, cap, fcol)


def solution(mesh):
    placed = (
        P("dp", None), P("dp", "mp"), P("dp", "mp"), P("dp", None), P("dp", None, None, None),
        P(), P(), P(None, "mp"), P("mp"), P("mp", None), P(), P(), P("dp", None), P("dp", None),
    )
    return jax.shard_map(
        functools.partial(per_device, mesh.shape["dp"], mesh.shape["mp"]),
        mesh=mesh,
        in_specs=placed,
        out_specs=(P("dp", "mp"), P("dp", "mp"), P("dp", "mp"), P("dp", None, None, "mp")),
        check_vma=False,
    )
```

time: 43.5 us -> 34.9 us (0.80)
  Pallas kernels: 42.7 us -> 34.1 us
    pallas_call x1, Pallas kernels: 40.4 us -> 33.1 us  [per_device(): pl.pallas_call(functools.partial(kernel, (n, mp, shard, rp, spread, cap,...]
    pallas_call x1, Pallas kernels: 2.26 us -> 1 us  [per_device(): pl.pallas_call(finish, out_shape=tuple((jax.ShapeDtypeStruct(x.shape, x.d...]
where the time goes in v2:
time: 34.9 us; the launch traced here: 34.7 us
  Pallas kernels  34.1 us (98%)
  between operations  0.64 us (2%)
    pallas_call x1, Pallas kernels, per_device(): pl.pallas_call(functools.partial(kernel, (n, mp, shard, rp, spread, cap,...  33.1 us
    pallas_call x1, Pallas kernels, per_device(): pl.pallas_call(finish, out_shape=tuple((jax.ShapeDtypeStruct(x.shape, x.d...  1 us

profile of v2, /device:TPU:0, one launch (start us, length us, event | category | flops | bytes accessed | tf_op | source)
XLA Modules:
  0.0 34.7 jit_solution(9591311355498290110)
XLA Ops:
  0.6 33.1 %shard_map.165 = (f32[449,128]{1,0:T(8,128)S(1)}, f32[449,128]{1,0:T(8,128)S(1)}, f32[449,256]{1,0:T(8,128)S(1)}, bf16[256,256]{1,0:T(8,128)(2,1)S(1)}) custom-call(bf16[512,3584]{1,0:T(8,128)(2,1)} %hid_h.1, bf16[512,128]{1,0:T(8,128)(2,1)} %key_h.1, bf16[512,128]{1,0:T(8,128)(2,1)} %val_h.1, bf16[256,1024]{1,0:T(8,128)(2,1)} %vis_h.1, ...), custom_call_target="tpu_custom_call" | custom-call | tf_op jit(solution)/shard_map/pallas_call | solution.py:537
  33.7 1.0 %shard_map.166 = (f32[449,128]{1,0:T(8,128)}, f32[449,128]{1,0:T(8,128)}, f32[449,256]{1,0:T(8,128)}, bf16[256,256]{1,0:T(8,128)(2,1)}) custom-call(f32[449,128]{1,0:T(8,128)S(1)} %get-tuple-element.12.refs_0_, f32[449,128]{1,0:T(8,128)S(1)} %get-tuple-element.13.refs_1_, f32[449,256]{1,0:T(8,128)S(1)} %get-tuple-element.14.refs_2_, ...), custom_call_target="tpu_custom_call" | custom-call | tf_op jit(solution)/shard_map/pallas_call | solution.py:591

commit v3 on v2

--- a/solution.py
+++ b/solution.py
@@ -38,12 +38,12 @@
     cot_mine, cot_recv,
     k0, k0r, k1, k1r, k2, k2r,
     v0, v0r, v1, v1r, v2, v2r,
-    z_full, z_own, z_send, z_recv, z_relay, pack, hbuf, acc, rs_send, rs_recv,
+    z_full, z_own, z_send, z_recv, z_relay, pack, hbuf,
     x1, x1r, x2, x2r, y1, y1r, y2, y2r,
     load_sem, cot_ss, cot_rs, z_ss, z_rs, e_ss, e_rs,
     k0_s, k0_r, k1_s, k1_r, k2_s, k2_r,
     v0_s, v0_r, v1_s, v1_r, v2_s, v2_r,
-    h_ss, h_rs, g_ss, g_rs, p_ss, p_rs,
+    h_ss, h_rs, g_ss, g_rs,
     x1_s, x1_r, x2_s, x2_r, y1_s, y1_r, y2_s, y2_r,
 ):
     n, mp, shard, rows_pad, spread, cap, nf, groups = cfg
@@ -357,14 +357,6 @@
             for j in range(1, nc):
                 share_copy(f, k, j).wait_recv()
 
-    offs = [(ja, jb) for jb in range(nb) for ja in range(na) if ja or jb]
-    offs.sort(key=lambda o: -((o[0] > 0) + (o[1] > 0)))
-
-    def rs_copy(i):
-        ja, jb = offs[i]
-        to = lax.rem(db + jb, nb) * na + lax.rem(da + ja, na)
-        return copy_to(rs_send.at[to], rs_recv.at[i], p_ss.at[i], p_rs.at[i], {"dp": to * nc + dc})
-
     def product_of(f, to):
         got = hbuf[f, dc].reshape(slots, fw)
         total = jnp.dot(cot_mine[dc, to], got, preferred_element_type=F32)
@@ -381,13 +373,25 @@
                 total = product_of(f, b * na + a).astype(BF)
                 x1[f, a, b] = total[:top]
                 y1[f, b, a] = total[top:]
-        return begin(x_first(f) + y_first(f))
-
-    def x_first(f):
-        return exchange(x1.at[f], x1r.at[f], x1_s.at[f], x1_r.at[f], da, na, at_a)
-
-    def y_first(f):
-        return exchange(y1.at[f], y1r.at[f], y1_s.at[f], y1_r.at[f], db, nb, at_b)
+        begin(x_first(f, True) + y_first(f, True))
+        begin(x_first(f, False) + y_first(f, False))
+
+    def first_stage(buf, got, ss, rs, digit, q, other, q2, peer_of, far):
+        cps = []
+        for j in range(1, q):
+            to = lax.rem(digit + j, q)
+            for i in range(1, q2) if far else (0,):
+                at = lax.rem(other + i, q2)
+                cps.append(
+                    copy_to(buf.at[to, at], got.at[j - 1, at], ss.at[j - 1, i], rs.at[j - 1, i], {"dp": peer_of(to)})
+                )
+        return cps
+
+    def x_first(f, far):
+        return first_stage(x1.at[f], x1r.at[f], x1_s.at[f], x1_r.at[f], da, na, db, nb, at_a, far)
+
+    def y_first(f, far):
+        return first_stage(y1.at[f], y1r.at[f], y1_s.at[f], y1_r.at[f], db, nb, da, na, at_b, far)
 
     def x_second(f):
         return exchange(x2.at[f], x2r.at[f], x2_s.at[f], x2_r.at[f], db, nb, at_b)
@@ -396,50 +400,50 @@
         return exchange(y2.at[f], y2r.at[f], y2_s.at[f], y2_r.at[f], da, na, at_a)
 
     def staged_next(f):
-        for cp in x_first(f):
+        for cp in x_first(f, True):
             cp.wait_recv()
-        for b in range(nb):
+        for j in range(1, nb):
+            b = lax.rem(db + j, nb)
             x2[f, b] = added(x1.at[f], x1r.at[f], da, na, (b,)).astype(BF)
         begin(x_second(f))
-        for cp in y_first(f):
+        for cp in y_first(f, True):
             cp.wait_recv()
-        for a in range(na):
+        for j in range(1, na):
+            a = lax.rem(da + j, na)
             y2[f, a] = added(y1.at[f], y1r.at[f], db, nb, (a,)).astype(BF)
         begin(y_second(f))
 
-    def direct(f):
-        for to in range(chips):
-            total = product_of(f, to)
-            acc[to] = total
-            rs_send[to] = total.astype(BF)
-        for i in range(len(offs)):
-            rs_copy(i).start()
-
     for f in range(1, nf):
         z_pass(f)
-    for f in range(nf):
+    s2k = exchange(k2, k2r, k2_s, k2_r, db, nb, at_b)
+    s2v = exchange(v2, v2r, v2_s, v2_r, da, na, at_a)
+
+    def key_third():
+        for g in range(groups):
+            for j in range(1, na):
+                k1_copy(j, g).wait_recv()
+        for b in range(nb):
+            k2[b] = added(k1, k1r, da, na, (b,)).astype(BF)
+        begin(s2k)
+
+    def value_third():
+        for j in range(1, nb):
+            v1_copy(j).wait_recv()
+        for a in range(na):
+            v2[a] = added(v1, v1r, db, nb, (a,)).astype(BF)
+        begin(s2v)
+
+    encode(0)
+    key_third()
+    for f in range(1, nf):
         encode(f)
-
-    for g in range(groups):
-        for j in range(1, na):
-            k1_copy(j, g).wait_recv()
-    for b in range(nb):
-        k2[b] = added(k1, k1r, da, na, (b,)).astype(BF)
-    s2k = begin(exchange(k2, k2r, k2_s, k2_r, db, nb, at_b))
-    for j in range(1, nb):
-        v1_copy(j).wait_recv()
-    for a in range(na):
-        v2[a] = added(v1, v1r, db, nb, (a,)).astype(BF)
-    s2v = begin(exchange(v2, v2r, v2_s, v2_r, da, na, at_a))
-
+    value_third()
     for cp in cot_cps:
         cp.wait_recv()
-    for f in range(nf - 1):
+    for f in range(nf):
         hand_wait(f)
         staged(f)
-    hand_wait(nf - 1)
-    direct(nf - 1)
-    for f in range(nf - 1):
+    for f in range(nf):
         staged_next(f)
 
     for f in range(nf):
@@ -450,30 +454,12 @@
     for cp in s2v:
         cp.wait_recv()
     val_o[...] = added(v2, v2r, da, na, ())[:shard]
-    total = acc[chip]
-    for i in range(len(offs)):
-        rs_copy(i).wait_recv()
-        total = total + rs_recv[i].astype(F32)
-    proj_o[:, (nf - 1) * fw :] = total[:shard]
-    for f in range(nf - 1):
-        for cp in x_second(f):
-            cp.wait_recv()
-        proj_o[:top, f * fw : (f + 1) * fw] = added(x2.at[f], x2r.at[f], db, nb, ())
-        for cp in y_second(f):
-            cp.wait_recv()
-        proj_o[top:, f * fw : (f + 1) * fw] = added(y2.at[f], y2r.at[f], da, na, ())[: shard - top]
-
     for f in range(nf):
         z_drain(f)
         for k in range(1, spread + 1):
             hand_copy(f, k).wait_send()
             for j in range(1, nc):
                 share_copy(f, k, j).wait_send()
-    for f in range(nf - 1):
-        for cp in x_first(f) + y_first(f) + x_second(f) + y_second(f):
-            cp.wait_send()
-    for i in range(len(offs)):
-        rs_copy(i).wait_send()
     for g in range(groups):
         for cp in kv_first(k0, k0r, k0_s, k0_r, g) + kv_first(v0, v0r, v0_s, v0_r, g):
             cp.wait_send()
@@ -483,6 +469,31 @@
         v1_copy(j).wait_send()
     for cp in cot_cps + s2k + s2v:
         cp.wait_send()
+    for f in range(nf):
+        for cp in x_first(f, True) + y_first(f, True) + x_first(f, False) + y_first(f, False):
+            cp.wait_send()
+
+    def kept(buf, first, second, digit, q, other, q2):
+        total = buf[digit, other].astype(F32)
+        for j in range(1, q):
+            total = total + first[j - 1, other].astype(F32)
+        for j in range(1, q2):
+            total = total + second[j - 1].astype(F32)
+        return total
+
+    for f in range(nf):
+        at = slice(f * fw, (f + 1) * fw)
+        for cp in x_first(f, False) + y_first(f, False):
+            cp.wait_recv()
+        for cp in x_second(f):
+            cp.wait_recv()
+        proj_o[:top, at] = kept(x1.at[f], x1r.at[f], x2r.at[f], da, na, db, nb)
+        for cp in y_second(f):
+            cp.wait_recv()
+        proj_o[top:, at] = kept(y1.at[f], y1r.at[f], y2r.at[f], db, nb, da, na)[: shard - top]
+    for f in range(nf):
+        for cp in x_second(f) + y_second(f):
+            cp.wait_send()
 
 
 def finish(*refs):
@@ -505,7 +516,7 @@
     spread, cap = visual_cotangent.shape[1:3]
     slots = spread * cap
     shard = (width + n) // n
-    rp = up(shard, 16)
+    rp = up(shard, 8)
     nc, na, nb = factors(n)
     chips = n // nc
     kc = key_grad.shape[1]
@@ -515,9 +526,9 @@
     fw = fcol // nf
     groups = 2 if nb % 2 == 0 else 1
     tall = up(max((n - 1) * shard + rp, width + 8), 8)
-    top = max(up(rp // 2, 16), 16)
-    low = max(rp - top, 16)
-    ns = max(nf - 1, 1)
+    top = up(rp // 2, 8)
+    low = max(rp - top, 8)
+    ns = nf
     any_spec = pl.BlockSpec(memory_space=pl.ANY)
     vm = pl.BlockSpec(memory_space=pltpu.VMEM)
     dma = lambda *s: pltpu.SemaphoreType.DMA(tuple(max(x, 1) for x in s))
@@ -568,9 +579,6 @@
             bf(nf, rows, fw),
             bf(nf, spread, cap, fw),
             bf(nf, nc, spread, cap, fw),
-            pltpu.VMEM((chips, rp, fw), F32),
-            bf(chips, rp, fw),
-            bf(chips - 1, rp, fw),
         ]
         + halves(na, nb, top)
         + halves(nb, na, low)
@@ -578,9 +586,8 @@
         + [dma(nc - 1, groups), dma(nc - 1, groups), dma(na - 1, groups), dma(na - 1, groups), dma(nb - 1), dma(nb - 1)]
         + [dma(nc - 1, groups), dma(nc - 1, groups), dma(nb - 1), dma(nb - 1), dma(na - 1), dma(na - 1)]
         + [dma(nf, spread), dma(nf, spread), dma(nf, spread, nc - 1), dma(nf, spread, nc - 1)]
-        + [dma(chips - 1), dma(chips - 1)]
-        + [dma(ns, q) for q in (na - 1, na - 1, nb - 1, nb - 1)]
-        + [dma(ns, q) for q in (nb - 1, nb - 1, na - 1, na - 1)],
+        + [dma(ns, na - 1, nb), dma(ns, na - 1, nb), dma(ns, nb - 1), dma(ns, nb - 1)]
+        + [dma(ns, nb - 1, na), dma(ns, nb - 1, na), dma(ns, na - 1), dma(ns, na - 1)],
         compiler_params=pltpu.CompilerParams(
             collective_id=0, has_side_effects=True, vmem_limit_bytes=56 * 1024 * 1024
         ),

time: 34.9 us -> 33.7 us (0.966)
  Pallas kernels: 34.1 us -> 32.9 us
    pallas_call x1, Pallas kernels: 33.1 us -> 31.9 us  [per_device(): pl.pallas_call(functools.partial(kernel, (n, mp, shard, rp, spread, cap,...]
where the time goes in v3:
time: 33.7 us; the launch traced here: 33.5 us
  Pallas kernels  32.9 us (98%)
  between operations  0.64 us (2%)
    pallas_call x1, Pallas kernels, per_device(): pl.pallas_call(functools.partial(kernel, (n, mp, shard, rp, spread, cap,...  31.9 us
    pallas_call x1, Pallas kernels, per_device(): pl.pallas_call(finish, out_shape=tuple((jax.ShapeDtypeStruct(x.shape, x.d...  1 us

profile of v3, /device:TPU:0, one launch (start us, length us, event | category | flops | bytes accessed | tf_op | source)
XLA Modules:
  0.0 33.5 jit_solution(2751980341528882648)
XLA Ops:
  0.6 31.9 %shard_map.165 = (f32[449,128]{1,0:T(8,128)S(1)}, f32[449,128]{1,0:T(8,128)S(1)}, f32[449,256]{1,0:T(8,128)S(1)}, bf16[256,256]{1,0:T(8,128)(2,1)S(1)}) custom-call(bf16[512,3584]{1,0:T(8,128)(2,1)} %hid_h.1, bf16[512,128]{1,0:T(8,128)(2,1)} %key_h.1, bf16[512,128]{1,0:T(8,128)(2,1)} %val_h.1, bf16[256,1024]{1,0:T(8,128)(2,1)} %vis_h.1, ...), custom_call_target="tpu_custom_call" | custom-call | tf_op jit(solution)/shard_map/pallas_call | solution.py:548
  32.5 1.0 %shard_map.166 = (f32[449,128]{1,0:T(8,128)}, f32[449,128]{1,0:T(8,128)}, f32[449,256]{1,0:T(8,128)}, bf16[256,256]{1,0:T(8,128)(2,1)}) custom-call(f32[449,128]{1,0:T(8,128)S(1)} %get-tuple-element.12.refs_0_, f32[449,128]{1,0:T(8,128)S(1)} %get-tuple-element.13.refs_1_, f32[449,256]{1,0:T(8,128)S(1)} %get-tuple-element.14.refs_2_, ...), custom_call_target="tpu_custom_call" | custom-call | tf_op jit(solution)/shard_map/pallas_call | solution.py:598

commit v4 on v3

--- a/solution.py
+++ b/solution.py
@@ -331,12 +331,15 @@
     def hand_copy(f, k):
         to = lax.rem(me + k, n)
         inside = lax.rem(to, nc)
-        return copy_to(pack.at[f, k - 1], hbuf.at[f, inside, k - 1], h_ss.at[f, k - 1], h_rs.at[f, k - 1], {"dp": to})
-
-    def share_copy(f, k, j):
+        return copy_to(pack.at[f, k - 1], hbuf.at[f, inside, k - 1], h_ss.at[f], h_rs.at[f], {"dp": to})
+
+    def hand_all(f):
+        return copy_to(pack.at[f], hbuf.at[f, dc], h_ss.at[f], h_rs.at[f], {"dp": lax.rem(me + 1, n)})
+
+    def share_copy(f, j):
         to = lax.rem(dc + j, nc)
-        block = hbuf.at[f, dc, k - 1]
-        return copy_to(block, block, g_ss.at[f, k - 1, j - 1], g_rs.at[f, k - 1, j - 1], {"dp": at_c(to)})
+        block = hbuf.at[f, dc]
+        return copy_to(block, block, g_ss.at[f, j - 1], g_rs.at[f, j - 1], {"dp": at_c(to)})
 
     def encode(f):
         z_sum(f)
@@ -349,13 +352,11 @@
             hand_copy(f, k).start()
 
     def hand_wait(f):
-        for k in range(1, spread + 1):
-            hand_copy(f, k).wait_recv()
-            for j in range(1, nc):
-                share_copy(f, k, j).start()
-        for k in range(1, spread + 1):
-            for j in range(1, nc):
-                share_copy(f, k, j).wait_recv()
+        hand_all(f).wait_recv()
+        for j in range(1, nc):
+            share_copy(f, j).start()
+        for j in range(1, nc):
+            share_copy(f, j).wait_recv()
 
     def product_of(f, to):
         got = hbuf[f, dc].reshape(slots, fw)
@@ -368,12 +369,17 @@
     top = x1.shape[-2]
 
     def staged(f):
-        for a in range(na):
-            for b in range(nb):
+        def fill(pairs):
+            for ja, jb in pairs:
+                a, b = lax.rem(da + ja, na), lax.rem(db + jb, nb)
                 total = product_of(f, b * na + a).astype(BF)
                 x1[f, a, b] = total[:top]
                 y1[f, b, a] = total[top:]
+
+        pairs = [(ja, jb) for ja in range(na) for jb in range(nb)]
+        fill([p for p in pairs if p[0] and p[1]])
         begin(x_first(f, True) + y_first(f, True))
+        fill([p for p in pairs if not (p[0] and p[1])])
         begin(x_first(f, False) + y_first(f, False))
 
     def first_stage(buf, got, ss, rs, digit, q, other, q2, peer_of, far):
@@ -456,10 +462,9 @@
     val_o[...] = added(v2, v2r, da, na, ())[:shard]
     for f in range(nf):
         z_drain(f)
-        for k in range(1, spread + 1):
-            hand_copy(f, k).wait_send()
-            for j in range(1, nc):
-                share_copy(f, k, j).wait_send()
+        hand_all(f).wait_send()
+        for j in range(1, nc):
+            share_copy(f, j).wait_send()
     for g in range(groups):
         for cp in kv_first(k0, k0r, k0_s, k0_r, g) + kv_first(v0, v0r, v0_s, v0_r, g):
             cp.wait_send()
@@ -585,7 +590,7 @@
         + [dma(14), dma(nc - 1), dma(nc - 1), dma(nf, mp - 1), dma(nf, mp - 1), dma(nf), dma(nf)]
         + [dma(nc - 1, groups), dma(nc - 1, groups), dma(na - 1, groups), dma(na - 1, groups), dma(nb - 1), dma(nb - 1)]
         + [dma(nc - 1, groups), dma(nc - 1, groups), dma(nb - 1), dma(nb - 1), dma(na - 1), dma(na - 1)]
-        + [dma(nf, spread), dma(nf, spread), dma(nf, spread, nc - 1), dma(nf, spread, nc - 1)]
+        + [dma(nf), dma(nf), dma(nf, nc - 1), dma(nf, nc - 1)]
         + [dma(ns, na - 1, nb), dma(ns, na - 1, nb), dma(ns, nb - 1), dma(ns, nb - 1)]
         + [dma(ns, nb - 1, na), dma(ns, nb - 1, na), dma(ns, na - 1), dma(ns, na - 1)],
         compiler_params=pltpu.CompilerParams(

time: 33.7 us -> 33.4 us (level)
  no operation moved by 1% of the time
where the time goes in v4:
time: 33.4 us; the launch traced here: 33.3 us
  Pallas kernels  32.6 us (98%)
  between operations  0.64 us (2%)
    pallas_call x1, Pallas kernels, per_device(): pl.pallas_call(functools.partial(kernel, (n, mp, shard, rp, spread, cap,...  31.6 us
    pallas_call x1, Pallas kernels, per_device(): pl.pallas_call(finish, out_shape=tuple((jax.ShapeDtypeStruct(x.shape, x.d...  1 us

profile of v4, /device:TPU:0, one launch (start us, length us, event | category | flops | bytes accessed | tf_op | source)
XLA Modules:
  0.0 33.3 jit_solution(3274277370971601425)
XLA Ops:
  0.6 31.6 %shard_map.165 = (f32[449,128]{1,0:T(8,128)S(1)}, f32[449,128]{1,0:T(8,128)S(1)}, f32[449,256]{1,0:T(8,128)S(1)}, bf16[256,256]{1,0:T(8,128)(2,1)S(1)}) custom-call(bf16[512,3584]{1,0:T(8,128)(2,1)} %hid_h.1, bf16[512,128]{1,0:T(8,128)(2,1)} %key_h.1, bf16[512,128]{1,0:T(8,128)(2,1)} %val_h.1, bf16[256,1024]{1,0:T(8,128)(2,1)} %vis_h.1, ...), custom_call_target="tpu_custom_call" | custom-call | tf_op jit(solution)/shard_map/pallas_call | solution.py:553
  32.3 1.0 %shard_map.166 = (f32[449,128]{1,0:T(8,128)}, f32[449,128]{1,0:T(8,128)}, f32[449,256]{1,0:T(8,128)}, bf16[256,256]{1,0:T(8,128)(2,1)}) custom-call(f32[449,128]{1,0:T(8,128)S(1)} %get-tuple-element.12.refs_0_, f32[449,128]{1,0:T(8,128)S(1)} %get-tuple-element.13.refs_1_, f32[449,256]{1,0:T(8,128)S(1)} %get-tuple-element.14.refs_2_, ...), custom_call_target="tpu_custom_call" | custom-call | tf_op jit(solution)/shard_map/pallas_call | solution.py:603
